TPU v7x, 32 devices: a whole 2x2x4 slice. The times are simulated.
32 devices in a mesh: tm: 2 (over y), space: 4 (over z), member: 4 (over x, core).
Axes of the slice: x: 2, y: 2, z: 4, core: 2. Of those that a mesh axis runs over, the one named last changes fastest.
Arguments:
- obs_anom: bfloat16 [6, 2, 8, 256, 1024], P('tm', None, 'space', 'member'), may hold values from -0.59375 to 0.59375
- obs_prec: bfloat16 [6, 2, 8, 1024], P('tm', None, 'space'), may hold values from 0.29882812 to 3
- innov: bfloat16 [6, 2, 8, 1024], P('tm', None, 'space'), may hold values from -6 to 6
- obs_column: int32 [6, 2, 8, 1024], P('tm', None, 'space'), may hold values from 0 to 127
- cutoff: int32 [2, 8], replicated, may hold values from 1 to 2
- inv_root: float32 [2, 8, 256, 256], P('tm', 'space'), may hold values from -0.12 to 0.12
- state_anom: bfloat16 [2, 8, 256, 32, 128], P('tm', 'space', None, 'member'), may hold values from -6 to 6
- state_mean: float32 [2, 8, 32, 128], P('tm', 'space', 'member'), may hold values from -6 to 6
Outputs:
- analysis: bfloat16 [2, 8, 256, 32, 128], P('tm', 'space', None, 'member')
All inputs are finite; a program needn't handle non-finite values.
Results may differ from a plain program's by a relative error of at most 0.0062.
Values may be sent and summed in bfloat16 or wider, within the bound.
A program may use at most 64 MiB of HBM per device.

v0:
```python
import math
import jax
import jax.numpy as jnp
from jax import lax
from jax.sharding import PartitionSpec as P

K = 256
HALO = 2
NEWTON = 2


def with_halo(cells, sides, width):
    for axis, dim in sides:
        count = lax.axis_size(axis)
        head = lax.slice_in_dim(cells, 0, width, axis=dim)
        tail = lax.slice_in_dim(cells, cells.shape[dim] - width, cells.shape[dim], axis=dim)
        cells = jnp.concatenate(
            [
                lax.ppermute(tail, axis, [(i, (i + 1) % count) for i in range(count)]),
                cells,
                lax.ppermute(head, axis, [((i + 1) % count, i) for i in range(count)]),
            ],
            axis=dim,
        )
    return cells


def taper_weight(distance, reach_now, columns):
    scaled_reach = (reach_now + 0.5) * columns
    relative = distance / scaled_reach
    return jnp.square(jnp.maximum(1.0 - relative * relative, 0.0))


def tile_cutoffs(cutoff, first_tile, how_many):
    flattened = cutoff.reshape(-1)
    cycle_size = flattened.shape[0]
    wanted = (first_tile + jnp.arange(how_many, dtype=jnp.int32) + cycle_size) % cycle_size
    matches = wanted[:, None] == jnp.arange(cycle_size, dtype=jnp.int32)[None, :]
    return jnp.sum(jnp.where(matches, flattened[None, :], 0), axis=1).astype(jnp.float32)


def spread_sums(relaid, reaches, shifts, columns):
    members = relaid.shape[2] - 3
    tile_count = relaid.shape[1]
    window_len = shifts.shape[0]
    extended = tile_count + window_len - 1
    start_gram = jnp.zeros((extended, members, members), jnp.float32)
    start_proj = jnp.zeros((extended, members), jnp.float32)

    def add_tile(tile_index, carry):
        gram_sums, proj_sums = carry
        obs_slab = lax.dynamic_index_in_dim(relaid, tile_index, 1, keepdims=False)
        anomaly = obs_slab[:, :members]
        precision = obs_slab[:, members].astype(jnp.float32)
        innovation = obs_slab[:, members + 1].astype(jnp.float32)
        placing = obs_slab[:, members + 2].astype(jnp.float32)
        reach_now = lax.dynamic_slice_in_dim(reaches, tile_index, window_len, 0)
        distance = shifts[:, None, None] * columns + placing[None]
        coeffs = taper_weight(distance, reach_now[:, None, None], columns) * precision[None]
        scaled = (anomaly[None] * coeffs[:, :, None, :]).astype(jnp.bfloat16)
        weighted = (coeffs * innovation[None]).astype(jnp.bfloat16)
        gram_part = jnp.einsum("wsko,slo->wkl", scaled, anomaly, preferred_element_type=jnp.float32)
        proj_part = jnp.einsum("sko,wso->wk", anomaly, weighted, preferred_element_type=jnp.float32)
        gram_sums = lax.dynamic_update_slice_in_dim(
            gram_sums,
            lax.dynamic_slice_in_dim(gram_sums, tile_index, window_len, 0) + gram_part,
            tile_index,
            0,
        )
        proj_sums = lax.dynamic_update_slice_in_dim(
            proj_sums,
            lax.dynamic_slice_in_dim(proj_sums, tile_index, window_len, 0) + proj_part,
            tile_index,
            0,
        )
        return (gram_sums, proj_sums)

    return lax.fori_loop(0, tile_count, add_tile, (start_gram, start_proj))


def body(obs_anom, obs_prec, innov, obs_column, cutoff, inv_root, state_anom, state_mean):
    columns = state_anom.shape[-1]
    placing = (obs_column.astype(jnp.float32) + (0.5 - columns / 2)).astype(jnp.bfloat16)
    obs_info = jnp.stack([obs_prec, innov, placing], axis=3)
    quarter = obs_anom.shape[4] // lax.axis_size("member")
    own_part = lax.dynamic_slice_in_dim(obs_info, lax.axis_index("member") * quarter, quarter, 4)
    ensemble = lax.all_to_all(obs_anom, "member", split_axis=4, concat_axis=3, tiled=True)
    combined = jnp.concatenate([ensemble, own_part], axis=3)
    relaid = lax.all_to_all(combined, "tm", split_axis=1, concat_axis=0, tiled=True)[:, 0]
    tile_count = relaid.shape[1]
    first_tile = (
        lax.axis_index("tm") * lax.axis_size("space") + lax.axis_index("space")
    ) * tile_count
    window_len = 2 * HALO + 1
    reaches = tile_cutoffs(cutoff, first_tile - HALO, tile_count + 2 * HALO)
    shifts = (HALO - jnp.arange(window_len, dtype=jnp.int32)).astype(jnp.float32)
    ext_gram, ext_proj = spread_sums(relaid, reaches, shifts, columns)
    stacked = jnp.concatenate([ext_gram, ext_proj[:, None, :]], axis=1)
    outgoing = jnp.concatenate([stacked[:HALO], stacked[tile_count + HALO :]], axis=0)
    arrived = with_halo(outgoing, ((("tm", "space"), 0),), HALO)
    owned = stacked[HALO : HALO + tile_count]
    owned = owned.at[:HALO].add(arrived[:HALO])
    owned = owned.at[tile_count - HALO :].add(arrived[3 * HALO :])
    gram_sums = owned[:, :K]
    proj_sums = owned[:, K]
    gram_sums, proj_sums = lax.psum((gram_sums, proj_sums), "member")
    highest = lax.Precision.HIGHEST
    identity = jnp.eye(K, dtype=jnp.float32)
    system = (K - 1.0) * identity + gram_sums
    inv_sqrt = inv_root[0]
    for newton_step in range(NEWTON):
        square = jnp.einsum("tij,tjk->tik", inv_sqrt, inv_sqrt, precision=highest)
        applied = jnp.einsum("tij,tjk->tik", system, square, precision=highest)
        inv_sqrt = 1.5 * inv_sqrt - 0.5 * jnp.einsum(
            "tij,tjk->tik", inv_sqrt, applied, precision=highest
        )
    inner_prod = jnp.einsum("tij,tj->ti", inv_sqrt, proj_sums, precision=highest)
    mean_weight = jnp.einsum("tij,tj->ti", inv_sqrt, inner_prod, precision=highest)
    weights = (mean_weight[:, :, None] + math.sqrt(K - 1) * inv_sqrt).astype(jnp.bfloat16)
    anomalies = state_anom[0].reshape(tile_count, K, -1)
    mean_rows = state_mean[0].reshape(tile_count, 1, -1)
    result = (
        jnp.einsum("tij,tiq->tjq", weights, anomalies, preferred_element_type=jnp.float32)
        + mean_rows
    )
    return result.astype(jnp.bfloat16).reshape(state_anom.shape)


def solution(mesh):
    in_specs = (
        P("tm", None, "space", "member", None),
        P("tm", None, "space", None),
        P("tm", None, "space", None),
        P("tm", None, "space", None),
        P(),
        P("tm", "space", None, None),
        P("tm", "space", None, "member", None),
        P("tm", "space", "member", None),
    )
    out_specs = P("tm", "space", None, "member", None)
    return jax.shard_map(body, mesh=mesh, in_specs=in_specs, out_specs=out_specs, check_vma=False)
```

profile of v0, /device:TPU:0, one launch (start us, length us, event | category | flops | bytes accessed | tf_op | source)
XLA Modules:
  0.0 166.9 jit_solution(3729697214545219223)
XLA Ops:
  6.5 7.3 %copy.73 = bf16[3,2,2,64,1024]{3,0,2,1,4:T(4,128)(2,1)} copy(bf16[3,2,2,64,1024]{4,3,2,1,0:T(8,128)(2,1)} %param.18) | data formatting | bytes 3145728 | tf_op args[0]
  13.9 5.5 %reshape.154 = bf16[4,2,98304]{2,1,0:T(2,128)(2,1)} reshape(bf16[1024,2,2,3,64]{4,3,2,1,0:T(4,128)(2,1)} %bitcast.100) | data formatting | bytes 3145728
  19.4 4.4 %all-to-all-start = ((bf16[4,2,98304]{2,1,0:T(2,128)(2,1)}), bf16[4,2,98304]{2,1,0:T(2,128)(2,1)S(1)}, u32[]{:S(2)}, u32[]{:S(2)}) async-start(bf16[4,2,98304]{2,1,0:T(2,128)(2,1)} %reshape.154), calls=%async_computation | async-start | bytes 3145728 | tf_op jit(solution)/shard_map/all_to_all | solution.py:87
  23.9 19.9 %all-to-all-done = bf16[4,2,98304]{2,1,0:T(2,128)(2,1)S(1)} async-done(((bf16[4,2,98304]{2,1,0:T(2,128)(2,1)}), bf16[4,2,98304]{2,1,0:T(2,128)(2,1)S(1)}, u32[]{:S(2)}, u32[]{:S(2)}) %all-to-all-start) | async-done | bytes 1572896 | tf_op jit(solution)/shard_map/all_to_all | solution.py:87
  43.8 3.8 %reshape.155 = bf16[1024,2,2,3,64]{4,3,2,1,0:T(4,128)(2,1)} reshape(bf16[4,2,98304]{2,1,0:T(2,128)(2,1)S(1)} %all-to-all-done) | data formatting | bytes 3145728
  47.6 9.8 %copy.74 = bf16[3,2,2,4,64,256]{5,2,4,3,0,1:T(2,128)(2,1)S(1)} copy(bf16[3,2,2,4,64,256]{4,0,2,1,5,3:T(4,128)(2,1)} %bitcast.99) | data formatting | bytes 3145728 | tf_op jit(solution)/shard_map/all_to_all | solution.py:87
  57.4 3.2 %pad_maximum_fusion = bf16[3,2,2,259,256]{4,2,3,0,1:T(2,128)(2,1)} fusion(bf16[3,2,2,3,256]{4,2,3,0,1:T(2,128)(2,1)S(1)} %fusion.35, bf16[3,2,2,256,256]{4,2,3,0,1:T(2,128)(2,1)S(1)} %bitcast.102), kind=kLoop, calls=%fused_computation.29 | loop fusion | flops 795648 | bytes 3182592 | tf_op jit(solution)/shard_map/concatenate | solution.py:88
  60.6 3.8 %all-to-all-start.1 = ((bf16[3,2,2,259,256]{4,2,3,0,1:T(2,128)(2,1)}), bf16[3,2,2,259,256]{4,2,3,0,1:T(2,128)(2,1)S(1)}, u32[]{:S(2)}, u32[]{:S(2)}) async-start(bf16[3,2,2,259,256]{4,2,3,0,1:T(2,128)(2,1)} %pad_maximum_fusion), calls=%async_computation.1 | async-start | bytes 3182592 | tf_op jit(solution)/shard_map/all_to_all | solution.py:89
  64.6 0.2 select_reduce_fusion
  64.8 19.6 %all-to-all-done.1 = bf16[3,2,2,259,256]{4,2,3,0,1:T(2,128)(2,1)S(1)} async-done(((bf16[3,2,2,259,256]{4,2,3,0,1:T(2,128)(2,1)}), bf16[3,2,2,259,256]{4,2,3,0,1:T(2,128)(2,1)S(1)}, u32[]{:S(2)}, u32[]{:S(2)}) %all-to-all-start.1) | async-done | bytes 1591328 | tf_op jit(solution)/shard_map/all_to_all | solution.py:89
  84.4 1.2 copy-done
  85.6 1.6 copy.78
  87.2 0.1 broadcast_in_dim.48
  87.3 4.5 %while.20 = (s32[]{:T(128)}, f32[6,256,256]{2,1,0:T(8,128)S(1)}, f32[6,256]{1,0:T(8,128)S(1)}, bf16[6,2,259,256]{3,2,0,1:T(8,128)(2,1)S(1)}, f32[6]{0:T(128)S(1)}, /*index=5*/s32[]{:T(128)}, s32[]{:T(128)}) while((s32[]{:T(128)}, f32[6,256,256]{2,1,0:T(8,128)S(1)}, f32[6,256]{1,0:T(8,128)S(1)}, ...), condition=%wide.region_2.3_spmd.clone, body=%wide.region_1.2_spmd.clone.sunk | while | flops 1015346944 | bytes 9977029 | solution.py:78
  87.5 0.1 convert_multiply_fusion.2
  87.5 0.1 multiply_multiply_fusion.3
  87.7 0.1 slice_convert_fusion.7
  87.8 1.4 fusion.60
  89.2 0.3 fusion.61
  89.8 0.1 multiply_multiply_fusion.3
  89.9 0.1 slice_convert_fusion.7
  90.1 1.4 fusion.60
  91.4 0.3 fusion.61
  91.9 0.1 constant_dynamic-update-slice_fusion
  92.1 0.1 fusion.42
  92.2 0.3 copy.79
  92.5 1.8 %collective-permute-start = (f32[2,257,256]{2,0,1:T(2,128)S(1)}, f32[2,257,256]{2,0,1:T(2,128)S(1)}, u32[]{:S(2)}, u32[]{:S(2)}) collective-permute-start(f32[2,257,256]{2,0,1:T(2,128)S(1)} %copy.79), channel_id=1, source_target_pairs={{0,4},{4,8},{8,12},{12,16},{16,20},{20,24},{24,28},{28,0},{1,5},{5... | collective-permute-start | bytes 1579016 | tf_op jit(solution)/shard_map/ppermute | solution.py:19
  94.3 0.3 copy.81
  94.6 3.0 %collective-permute-start.1 = (f32[2,257,256]{2,0,1:T(2,128)S(1)}, f32[2,257,256]{2,0,1:T(2,128)S(1)}, u32[]{:S(2)}, u32[]{:S(2)}) collective-permute-start(f32[2,257,256]{2,0,1:T(2,128)S(1)} %copy.81), channel_id=1, source_target_pairs={{4,0},{8,4},{12,8},{16,12},{20,16},{24,20},{28,24},{0,28},{5,1},{9... | collective-permute-start | bytes 1579016 | tf_op jit(solution)/shard_map/ppermute | solution.py:21
  97.6 12.5 %collective-permute-done = f32[2,257,256]{2,0,1:T(2,128)S(1)} collective-permute-done((f32[2,257,256]{2,0,1:T(2,128)S(1)}, f32[2,257,256]{2,0,1:T(2,128)S(1)}, u32[]{:S(2)}, u32[]{:S(2)}) %collective-permute-start) | collective-permute-done | bytes 526368 | tf_op jit(solution)/shard_map/ppermute | solution.py:19
  110.1 8.2 %collective-permute-done.1 = f32[2,257,256]{2,0,1:T(2,128)S(1)} collective-permute-done((f32[2,257,256]{2,0,1:T(2,128)S(1)}, f32[2,257,256]{2,0,1:T(2,128)S(1)}, u32[]{:S(2)}, u32[]{:S(2)}) %collective-permute-start.1) | collective-permute-done | bytes 526368 | tf_op jit(solution)/shard_map/ppermute | solution.py:21
  118.2 0.1 fusion.18
  118.3 0.9 slice.97
  119.3 0.2 copy.72
  119.5 1.5 reshape_squeeze.4
  121.1 0.6 fusion.19
  121.7 0.7 slice.98
  122.5 6.4 %psum.15 = f32[2,256]{1,0:T(2,128)S(1)} all-reduce(f32[2,256]{1,0:T(2,128)S(1)} %bitcast.109), channel_id=1, replica_groups=mesh['tm'=2,'space'=4,'member'=4] {'member'}, use_global_device_ids=true, to_apply=%region_4.5 | all-reduce | flops 512 | bytes 4096 | tf_op jit(solution)/shard_map/psum | solution.py:106
  128.8 23.1 %all-reduce.2.cloned.1.call-done = f32[2,256,256]{2,1,0:T(8,128)} async-done(((f32[2,256,256]{2,1,0:T(8,128)}), f32[2,256,256]{2,1,0:T(8,128)}) %all-reduce.2.cloned.1.call-update) | async-done | bytes 524304 | tf_op jit(solution)/shard_map/psum | solution.py:106
  151.9 2.1 %fusion.24 = f32[2,256,256]{1,2,0:T(8,128)S(1)} fusion(f32[2,256,256]{2,1,0:T(8,128)S(1)} %fusion.19, f32[2,256,256]{2,1,0:T(8,128)} %all-reduce.2.cloned.1.call-done, f32[256,256]{1,0:T(8,128)S(1)} %fusion.30), kind=kOutput, calls=%fused_computation.44 | convolution fusion | flops 402784256 | bytes 1835008 | tf_op jit(solution)/shard_map/tij,tjk->tik/dot_general | solution.py:113
  154.0 0.7 fusion.17
  154.7 1.1 fusion.43
  155.8 0.7 fusion.22
  156.5 1.1 fusion.15
  157.5 0.4 fusion.38
  157.9 0.4 fusion.36
  158.3 0.5 add_convert_fusion
  158.8 1.2 copy.116
  (46 shorter events, 0.9 us)
Async XLA Ops:
  19.4 4.4 %copy-start.4 = (s32[3,2,2,1024]{3,2,1,0:T(2,128)S(1)}, s32[3,2,2,1024]{3,2,1,0:T(2,128)}, u32[]{:S(2)}) copy-start(s32[3,2,2,1024]{3,2,1,0:T(2,128)} %param.21) | copy-start | bytes 147460
  19.4 4.4 %copy-start.5 = (bf16[3,2,2,1024]{3,2,1,0:T(2,128)(2,1)S(1)}, bf16[3,2,2,1024]{3,2,1,0:T(2,128)(2,1)}, u32[]{:S(2)}) copy-start(bf16[3,2,2,1024]{3,2,1,0:T(2,128)(2,1)} %param.20) | copy-start | bytes 73732
  19.4 4.4 %copy-start.6 = (bf16[3,2,2,1024]{3,2,1,0:T(2,128)(2,1)S(1)}, bf16[3,2,2,1024]{3,2,1,0:T(2,128)(2,1)}, u32[]{:S(2)}) copy-start(bf16[3,2,2,1024]{3,2,1,0:T(2,128)(2,1)} %param.19) | copy-start | bytes 73732
  19.4 24.4 %all-to-all-start = ((bf16[4,2,98304]{2,1,0:T(2,128)(2,1)}), bf16[4,2,98304]{2,1,0:T(2,128)(2,1)S(1)}, u32[]{:S(2)}, u32[]{:S(2)}) async-start(bf16[4,2,98304]{2,1,0:T(2,128)(2,1)} %reshape.154), calls=%async_computation | async-start | bytes 3145728 | tf_op jit(solution)/shard_map/all_to_all | solution.py:87
  60.6 3.9 %copy-start.8 = (s32[2,8]{1,0:T(2,128)S(1)}, s32[2,8]{1,0:T(2,128)}, u32[]{:S(2)}) copy-start(s32[2,8]{1,0:T(2,128)} %param.22) | copy-start | bytes 196
  60.6 23.7 %all-to-all-start.1 = ((bf16[3,2,2,259,256]{4,2,3,0,1:T(2,128)(2,1)}), bf16[3,2,2,259,256]{4,2,3,0,1:T(2,128)(2,1)S(1)}, u32[]{:S(2)}, u32[]{:S(2)}) async-start(bf16[3,2,2,259,256]{4,2,3,0,1:T(2,128)(2,1)} %pad_maximum_fusion), calls=%async_computation.1 | async-start | bytes 3182592 | tf_op jit(solution)/shard_map/all_to_all | solution.py:89
  64.4 87.5 %all-reduce.2.cloned.1.call-start = ((), (), s32[]{:S(2)}) async-start(), calls=%async_computation.2 | async-start | bytes 1048576 | tf_op jit(solution)/shard_map/psum | solution.py:106
  84.4 1.2 copy-start
  92.5 17.6 %collective-permute-start = (f32[2,257,256]{2,0,1:T(2,128)S(1)}, f32[2,257,256]{2,0,1:T(2,128)S(1)}, u32[]{:S(2)}, u32[]{:S(2)}) collective-permute-start(f32[2,257,256]{2,0,1:T(2,128)S(1)} %copy.79), channel_id=1, source_target_pairs={{0,4},{4,8},{8,12},{12,16},{16,20},{20,24},{24,28},{28,0},{1,5},{5... | collective-permute-start | bytes 1579016 | tf_op jit(solution)/shard_map/ppermute | solution.py:19
  94.6 24.7 %copy-start.1 = (f32[1,2,256,256]{3,2,1,0:T(8,128)S(1)}, f32[1,2,256,256]{3,2,1,0:T(8,128)}, u32[]{:S(2)}) copy-start(f32[1,2,256,256]{3,2,1,0:T(8,128)} %param.23) | copy-start | bytes 1572868
  94.6 23.6 %collective-permute-start.1 = (f32[2,257,256]{2,0,1:T(2,128)S(1)}, f32[2,257,256]{2,0,1:T(2,128)S(1)}, u32[]{:S(2)}, u32[]{:S(2)}) collective-permute-start(f32[2,257,256]{2,0,1:T(2,128)S(1)} %copy.81), channel_id=1, source_target_pairs={{4,0},{8,4},{12,8},{16,12},{20,16},{24,20},{28,24},{0,28},{5,1},{9... | collective-permute-start | bytes 1579016 | tf_op jit(solution)/shard_map/ppermute | solution.py:21
  118.3 1.0 copy-start.2
  119.3 1.7 %copy-start.7 = (f32[1,2,8,128]{3,2,1,0:T(8,128)S(1)}, f32[1,2,8,128]{3,2,1,0:T(8,128)}, u32[]{:S(2)}) copy-start(f32[1,2,8,128]{3,2,1,0:T(8,128)} %param.25) | copy-start | bytes 24580
  154.0 1.8 %copy-start.3 = (f32[2,256,256]{2,1,0:T(8,128)S(1)}, f32[2,256,256]{2,1,0:T(8,128)}, u32[]{:S(2)}) copy-start(f32[2,256,256]{2,1,0:T(8,128)} %all-reduce.2.cloned.1.call-done) | copy-start | bytes 1572868
Sparse Core Ops, SparseCore 0:
  119.4 32.4 all-reduce.1
where the time goes:
time: 168 us; the launch traced here: 167 us
  waiting for transfers between devices  83.2 us (50%)
  local copies, waits for them, and re-layouts  35.3 us (21%)
  between operations  13.7 us (8%)
  starting transfers between devices  13 us (8%)
  matrix products  10.8 us (6%)
  blocking collectives  6.37 us (4%)
  other arithmetic  4.26 us (3%)
    psum x1, waiting for transfers between devices, body(): gram_sums, proj_sums = lax.psum((gram_sums, proj_sums), 'member')  23.1 us
    unnamed x27, local copies, waits for them, and re-layouts  21.1 us
    all_to_all x1, waiting for transfers between devices, body(): lax.all_to_all(obs_anom, 'member', split_axis=4, concat_axis=3, tiled=True)  19.9 us
    all_to_all x1, waiting for transfers between devices, body(): lax.all_to_all(combined, 'tm', split_axis=1, concat_axis=0, tiled=True)  19.6 us
    ppermute x1, waiting for transfers between devices, with_halo(): lax.ppermute(tail, axis, [(i, (i + 1) % count) for i in range(count)])  12.5 us
    all_to_all x1, local copies, waits for them, and re-layouts, body(): lax.all_to_all(obs_anom, 'member', split_axis=4, concat_axis=3, tiled=True)  9.78 us
    ppermute x1, waiting for transfers between devices, with_halo(): lax.ppermute(head, axis, [((i + 1) % count, i) for i in range(count)])  8.16 us
    psum x1, blocking collectives, body(): gram_sums, proj_sums = lax.psum((gram_sums, proj_sums), 'member')  6.37 us
  transfers between devices with their start and end apart: 5, of which 5 were waited for; matrix products, arithmetic and copies ran while one was open for 2% of the time, Pallas kernels for 0%

commit v1 on v0

--- a/solution.py
+++ b/solution.py
@@ -84,7 +84,10 @@
     obs_info = jnp.stack([obs_prec, innov, placing], axis=3)
     quarter = obs_anom.shape[4] // lax.axis_size("member")
     own_part = lax.dynamic_slice_in_dim(obs_info, lax.axis_index("member") * quarter, quarter, 4)
-    ensemble = lax.all_to_all(obs_anom, "member", split_axis=4, concat_axis=3, tiled=True)
+    size = lax.axis_size("member")
+    shards = jnp.stack(jnp.split(obs_anom, size, axis=4), axis=0)
+    shards = lax.all_to_all(shards, "member", split_axis=0, concat_axis=0)
+    ensemble = jnp.concatenate(shards, axis=3)
     combined = jnp.concatenate([ensemble, own_part], axis=3)
     relaid = lax.all_to_all(combined, "tm", split_axis=1, concat_axis=0, tiled=True)[:, 0]
     tile_count = relaid.shape[1]

time: 168 us -> 143 us (0.85)
  local copies, waits for them, and re-layouts: 35.3 us -> 11.1 us
    unnamed x27 -> x23, local copies, waits for them, and re-layouts: 21.1 us -> 2.14 us
    all_to_all x1, local copies, waits for them, and re-layouts: 9.78 us -> 0.1 us  [body(): shards = lax.all_to_all(shards, 'member', split_axis=0, concat_axis=0)]
    concatenate x1, other arithmetic: 3.23 us -> 0.12 us  [body(): combined = jnp.concatenate([ensemble, own_part], axis=3)]
    concatenate x0 -> x1, local copies, waits for them, and re-layouts: none -> 2.37 us  [body(): combined = jnp.concatenate([ensemble, own_part], axis=3)]
where the time goes in v1:
time: 143 us; the launch traced here: 142 us
  waiting for transfers between devices  83.3 us (58%)
  starting transfers between devices  14 us (10%)
  between operations  13.7 us (10%)
  local copies, waits for them, and re-layouts  11.1 us (8%)
  matrix products  10.8 us (8%)
  blocking collectives  6.81 us (5%)
  other arithmetic  2.6 us (2%)
    psum x1, waiting for transfers between devices, body(): gram_sums, proj_sums = lax.psum((gram_sums, proj_sums), 'member')  23.2 us
    all_to_all x1, waiting for transfers between devices, body(): shards = lax.all_to_all(shards, 'member', split_axis=0, concat_axis=0)  19.7 us
    all_to_all x1, waiting for transfers between devices, body(): lax.all_to_all(combined, 'tm', split_axis=1, concat_axis=0, tiled=True)  19.7 us
    ppermute x1, waiting for transfers between devices, with_halo(): lax.ppermute(tail, axis, [(i, (i + 1) % count) for i in range(count)])  12.5 us
    ppermute x1, waiting for transfers between devices, with_halo(): lax.ppermute(head, axis, [((i + 1) % count, i) for i in range(count)])  8.13 us
    psum x1, blocking collectives, body(): gram_sums, proj_sums = lax.psum((gram_sums, proj_sums), 'member')  6.81 us
    all_to_all x1, starting transfers between devices, body(): lax.all_to_all(combined, 'tm', split_axis=1, concat_axis=0, tiled=True)  4.77 us
    all_to_all x1, starting transfers between devices, body(): shards = lax.all_to_all(shards, 'member', split_axis=0, concat_axis=0)  4.37 us
  transfers between devices with their start and end apart: 5, of which 5 were waited for; matrix products, arithmetic and copies ran while one was open for 2% of the time, Pallas kernels for 0%

profile of v1, /device:TPU:0, one launch (start us, length us, event | category | flops | bytes accessed | tf_op | source)
XLA Modules:
  0.0 142.5 jit_solution(11233062176115798018)
XLA Ops:
  6.5 1.5 %slice_bitcast_fusion.3 = (bf16[1,3,2,2,64,256]{5,4,3,2,1,0:T(8,128)(2,1)S(1)}, bf16[1,3,2,2,64,256]{5,4,3,2,1,0:T(8,128)(2,1)S(1)}, bf16[1,3,2,2,64,256]{5,4,3,...) fusion(bf16[3,2,2,64,1024]{4,3,2,1,0:T(8,128)(2,1)} %param.18), kind=kLoop, calls=%fused_computation.50 | loop fusion | bytes 3145728 | tf_op jit(solution)/shard_map/stack | solution.py:88
  8.0 1.4 pad_maximum_fusion.1
  9.4 4.4 %all-to-all-start = ((bf16[4,3,2,2,64,256]{5,4,3,2,1,0:T(8,128)(2,1)}), bf16[4,3,2,2,64,256]{5,4,3,2,1,0:T(8,128)(2,1)S(1)}, u32[]{:S(2)}, u32[]{:S(2)}) async-start(bf16[4,3,2,2,64,256]{5,4,3,2,1,0:T(8,128)(2,1)} %pad_maximum_fusion.1), calls=%async_computation | async-start | bytes 3145728 | tf_op jit(solution)/shard_map/all_to_all | solution.py:89
  13.9 0.1 fusion.32
  14.1 19.7 %all-to-all-done = bf16[4,3,2,2,64,256]{5,4,3,2,1,0:T(8,128)(2,1)S(1)} async-done(((bf16[4,3,2,2,64,256]{5,4,3,2,1,0:T(8,128)(2,1)}), bf16[4,3,2,2,64,256]{5,4,3,2,1,0:T(8,128)(2,1)S(1)}, u32[]{:S(2)}, u32[]{:S(2)}) %all-to-all-start) | async-done | bytes 1572896 | tf_op jit(solution)/shard_map/all_to_all | solution.py:89
  33.8 0.1 copy.85
  33.9 0.1 pad_maximum_fusion
  34.0 2.4 %copy.89 = bf16[3,2,2,259,256]{4,2,3,0,1:T(2,128)(2,1)} copy(bf16[3,2,2,259,256]{4,3,2,1,0:T(8,128)(2,1)S(1)} %pad_maximum_fusion) | data formatting | bytes 3182592 | tf_op jit(solution)/shard_map/concatenate | solution.py:91
  36.4 4.8 %all-to-all-start.1 = ((bf16[3,2,2,259,256]{4,2,3,0,1:T(2,128)(2,1)}), bf16[3,2,2,259,256]{4,2,3,0,1:T(2,128)(2,1)}, u32[]{:S(2)}, u32[]{:S(2)}) async-start(bf16[3,2,2,259,256]{4,2,3,0,1:T(2,128)(2,1)} %copy.89), calls=%async_computation.1 | async-start | bytes 3182592 | tf_op jit(solution)/shard_map/all_to_all | solution.py:92
  41.3 0.2 select_reduce_fusion
  41.5 19.7 %all-to-all-done.1 = bf16[3,2,2,259,256]{4,2,3,0,1:T(2,128)(2,1)} async-done(((bf16[3,2,2,259,256]{4,2,3,0,1:T(2,128)(2,1)}), bf16[3,2,2,259,256]{4,2,3,0,1:T(2,128)(2,1)}, u32[]{:S(2)}, u32[]{:S(2)}) %all-to-all-start.1) | async-done | bytes 1591328 | tf_op jit(solution)/shard_map/all_to_all | solution.py:92
  61.2 1.6 %copy.118 = bf16[3,2,2,259,256]{4,3,0,1,2:T(8,128)(2,1)S(1)} copy(bf16[3,2,2,259,256]{4,2,3,0,1:T(2,128)(2,1)} %all-to-all-done.1) | data formatting | bytes 3182592 | tf_op jit(solution)/shard_map/squeeze | solution.py:92
  62.9 0.1 broadcast_in_dim.48
  63.0 4.5 %while.20 = (s32[]{:T(128)}, f32[6,256,256]{2,1,0:T(8,128)S(1)}, f32[6,256]{1,0:T(8,128)S(1)}, bf16[6,2,259,256]{3,2,0,1:T(8,128)(2,1)S(1)}, f32[6]{0:T(128)S(1)}, /*index=5*/s32[]{:T(128)}, s32[]{:T(128)}) while((s32[]{:T(128)}, f32[6,256,256]{2,1,0:T(8,128)S(1)}, f32[6,256]{1,0:T(8,128)S(1)}, ...), condition=%wide.region_2.3_spmd.clone, body=%wide.region_1.2_spmd.clone.sunk | while | flops 1015346944 | bytes 9977029 | solution.py:78
  63.2 0.1 multiply_multiply_fusion.3
  63.3 0.1 slice_convert_fusion.7
  63.5 1.4 fusion.58
  64.8 0.3 fusion.59
  65.5 0.1 multiply_multiply_fusion.3
  65.6 0.1 slice_convert_fusion.7
  65.7 1.4 fusion.58
  67.1 0.3 fusion.59
  67.5 0.1 constant_dynamic-update-slice_fusion
  67.8 0.1 fusion.40
  67.9 0.3 copy.92
  68.1 1.8 %collective-permute-start = (f32[2,257,256]{2,0,1:T(2,128)S(1)}, f32[2,257,256]{2,0,1:T(2,128)S(1)}, u32[]{:S(2)}, u32[]{:S(2)}) collective-permute-start(f32[2,257,256]{2,0,1:T(2,128)S(1)} %copy.92), channel_id=1, source_target_pairs={{0,4},{4,8},{8,12},{12,16},{16,20},{20,24},{24,28},{28,0},{1,5},{5... | collective-permute-start | bytes 1579016 | tf_op jit(solution)/shard_map/ppermute | solution.py:19
  70.0 0.3 copy.94
  70.3 3.0 %collective-permute-start.1 = (f32[2,257,256]{2,0,1:T(2,128)S(1)}, f32[2,257,256]{2,0,1:T(2,128)S(1)}, u32[]{:S(2)}, u32[]{:S(2)}) collective-permute-start(f32[2,257,256]{2,0,1:T(2,128)S(1)} %copy.94), channel_id=1, source_target_pairs={{4,0},{8,4},{12,8},{16,12},{20,16},{24,20},{28,24},{0,28},{5,1},{9... | collective-permute-start | bytes 1579016 | tf_op jit(solution)/shard_map/ppermute | solution.py:21
  73.3 12.5 %collective-permute-done = f32[2,257,256]{2,0,1:T(2,128)S(1)} collective-permute-done((f32[2,257,256]{2,0,1:T(2,128)S(1)}, f32[2,257,256]{2,0,1:T(2,128)S(1)}, u32[]{:S(2)}, u32[]{:S(2)}) %collective-permute-start) | collective-permute-done | bytes 526368 | tf_op jit(solution)/shard_map/ppermute | solution.py:19
  85.7 8.1 %collective-permute-done.1 = f32[2,257,256]{2,0,1:T(2,128)S(1)} collective-permute-done((f32[2,257,256]{2,0,1:T(2,128)S(1)}, f32[2,257,256]{2,0,1:T(2,128)S(1)}, u32[]{:S(2)}, u32[]{:S(2)}) %collective-permute-start.1) | collective-permute-done | bytes 526368 | tf_op jit(solution)/shard_map/ppermute | solution.py:21
  93.9 0.1 fusion.18
  94.0 0.8 slice.97
  95.0 0.2 copy.84
  95.2 0.4 copy-done.3
  95.6 0.5 reshape_squeeze.4
  96.1 0.6 fusion.19
  96.8 0.7 slice.98
  97.5 6.8 %psum.15 = f32[2,256]{1,0:T(2,128)S(1)} all-reduce(f32[2,256]{1,0:T(2,128)S(1)} %bitcast.111), channel_id=1, replica_groups=mesh['tm'=2,'space'=4,'member'=4] {'member'}, use_global_device_ids=true, to_apply=%region_4.5 | all-reduce | flops 512 | bytes 4096 | tf_op jit(solution)/shard_map/psum | solution.py:109
  104.3 23.2 %all-reduce.2.cloned.1.call-done = f32[2,256,256]{2,1,0:T(8,128)} async-done(((f32[2,256,256]{2,1,0:T(8,128)}), f32[2,256,256]{2,1,0:T(8,128)}) %all-reduce.2.cloned.1.call-update) | async-done | bytes 524304 | tf_op jit(solution)/shard_map/psum | solution.py:109
  127.5 2.1 %fusion.24 = f32[2,256,256]{1,2,0:T(8,128)S(1)} fusion(f32[2,256,256]{2,1,0:T(8,128)S(1)} %fusion.19, f32[2,256,256]{2,1,0:T(8,128)} %all-reduce.2.cloned.1.call-done, f32[256,256]{1,0:T(8,128)S(1)} %fusion.30), kind=kOutput, calls=%fused_computation.45 | convolution fusion | flops 402784256 | bytes 1835008 | tf_op jit(solution)/shard_map/tij,tjk->tik/dot_general | solution.py:116
  129.6 0.7 fusion.17
  130.3 1.1 fusion.41
  131.4 0.7 fusion.22
  132.1 1.1 fusion.15
  133.1 0.4 fusion.36
  133.5 0.4 fusion.34
  133.9 0.5 add_convert_fusion
  134.4 1.2 copy.130
  (48 shorter events, 1.0 us)
Async XLA Ops:
  9.4 4.4 %copy-start.4 = (s32[3,2,2,1024]{3,2,1,0:T(2,128)S(1)}, s32[3,2,2,1024]{3,2,1,0:T(2,128)}, u32[]{:S(2)}) copy-start(s32[3,2,2,1024]{3,2,1,0:T(2,128)} %param.21) | copy-start | bytes 147460
  9.4 4.5 %copy-start.5 = (bf16[3,2,2,1024]{3,2,1,0:T(2,128)(2,1)S(1)}, bf16[3,2,2,1024]{3,2,1,0:T(2,128)(2,1)}, u32[]{:S(2)}) copy-start(bf16[3,2,2,1024]{3,2,1,0:T(2,128)(2,1)} %param.19) | copy-start | bytes 73732
  9.4 4.5 %copy-start.6 = (bf16[3,2,2,1024]{3,2,1,0:T(2,128)(2,1)S(1)}, bf16[3,2,2,1024]{3,2,1,0:T(2,128)(2,1)}, u32[]{:S(2)}) copy-start(bf16[3,2,2,1024]{3,2,1,0:T(2,128)(2,1)} %param.20) | copy-start | bytes 73732
  9.4 24.4 %all-to-all-start = ((bf16[4,3,2,2,64,256]{5,4,3,2,1,0:T(8,128)(2,1)}), bf16[4,3,2,2,64,256]{5,4,3,2,1,0:T(8,128)(2,1)S(1)}, u32[]{:S(2)}, u32[]{:S(2)}) async-start(bf16[4,3,2,2,64,256]{5,4,3,2,1,0:T(8,128)(2,1)} %pad_maximum_fusion.1), calls=%async_computation | async-start | bytes 3145728 | tf_op jit(solution)/shard_map/all_to_all | solution.py:89
  36.4 4.8 %copy-start.8 = (s32[2,8]{1,0:T(2,128)S(1)}, s32[2,8]{1,0:T(2,128)}, u32[]{:S(2)}) copy-start(s32[2,8]{1,0:T(2,128)} %param.22) | copy-start | bytes 196
  36.4 24.8 %all-to-all-start.1 = ((bf16[3,2,2,259,256]{4,2,3,0,1:T(2,128)(2,1)}), bf16[3,2,2,259,256]{4,2,3,0,1:T(2,128)(2,1)}, u32[]{:S(2)}, u32[]{:S(2)}) async-start(bf16[3,2,2,259,256]{4,2,3,0,1:T(2,128)(2,1)} %copy.89), calls=%async_computation.1 | async-start | bytes 3182592 | tf_op jit(solution)/shard_map/all_to_all | solution.py:92
  41.2 86.3 %all-reduce.2.cloned.1.call-start = ((), (), s32[]{:S(2)}) async-start(), calls=%async_computation.2 | async-start | bytes 1048576 | tf_op jit(solution)/shard_map/psum | solution.py:109
  68.1 17.6 %collective-permute-start = (f32[2,257,256]{2,0,1:T(2,128)S(1)}, f32[2,257,256]{2,0,1:T(2,128)S(1)}, u32[]{:S(2)}, u32[]{:S(2)}) collective-permute-start(f32[2,257,256]{2,0,1:T(2,128)S(1)} %copy.92), channel_id=1, source_target_pairs={{0,4},{4,8},{8,12},{12,16},{16,20},{20,24},{24,28},{28,0},{1,5},{5... | collective-permute-start | bytes 1579016 | tf_op jit(solution)/shard_map/ppermute | solution.py:19
  70.3 24.7 %copy-start = (f32[1,2,256,256]{3,2,1,0:T(8,128)S(1)}, f32[1,2,256,256]{3,2,1,0:T(8,128)}, u32[]{:S(2)}) copy-start(f32[1,2,256,256]{3,2,1,0:T(8,128)} %param.23) | copy-start | bytes 1572868
  70.3 23.6 %collective-permute-start.1 = (f32[2,257,256]{2,0,1:T(2,128)S(1)}, f32[2,257,256]{2,0,1:T(2,128)S(1)}, u32[]{:S(2)}, u32[]{:S(2)}) collective-permute-start(f32[2,257,256]{2,0,1:T(2,128)S(1)} %copy.94), channel_id=1, source_target_pairs={{4,0},{8,4},{12,8},{16,12},{20,16},{24,20},{28,24},{0,28},{5,1},{9... | collective-permute-start | bytes 1579016 | tf_op jit(solution)/shard_map/ppermute | solution.py:21
  94.0 1.0 copy-start.1
  94.0 1.6 %copy-start.3 = (bf16[1,2,256,8,128]{4,3,2,1,0:T(8,128)(2,1)S(1)}, bf16[1,2,256,8,128]{4,3,2,1,0:T(8,128)(2,1)}, u32[]{:S(2)}) copy-start(bf16[1,2,256,8,128]{4,3,2,1,0:T(8,128)(2,1)} %param.24) | copy-start | bytes 3145732
  95.0 1.1 copy-start.7
  129.6 1.8 %copy-start.2 = (f32[2,256,256]{2,1,0:T(8,128)S(1)}, f32[2,256,256]{2,1,0:T(8,128)}, u32[]{:S(2)}) copy-start(f32[2,256,256]{2,1,0:T(8,128)} %all-reduce.2.cloned.1.call-done) | copy-start | bytes 1572868
Sparse Core Ops, SparseCore 0:
  95.0 32.4 all-reduce.1
